TPU v7x, 32 devices: a whole 2x2x4 slice. The times are simulated.
32 devices in a mesh: row: 4 (over y, x), col: 8 (over z, core).
Axes of the slice: x: 2, y: 2, z: 4, core: 2. Of those that a mesh axis runs over, the one named last changes fastest.
Arguments:
- points: bfloat16 [10240, 64], P(('row', 'col')), may hold values from -5 to 5
- start_vectors: bfloat16 [10240, 32], P(('row', 'col')), may hold values from -12 to 12
Outputs:
- basis: float32 [10240, 32], P(('row', 'col'))
All inputs are finite; a program needn't handle non-finite values.
Results may differ from a plain program's by a relative error of at most 0.007.
Values may be sent and summed in bfloat16 or wider, within the bound.
A program may use at most 64 MiB of HBM per device.

v0:
```python
import jax
import jax.numpy as jnp
from jax import lax
from jax.sharding import PartitionSpec as P

ITERS = 2
KERNEL_SCALE = 5.12


def squared_norms(values):
    return jnp.sum(jnp.square(values.astype(jnp.float32)), axis=1)


def affinity(block_pts, block_sq, col_pts, col_sq):
    features = block_pts.shape[1]
    cross = lax.dot_general(
        block_pts, col_pts, (((1,), (1,)), ((), ())), preferred_element_type=jnp.float32
    )
    dist = block_sq[:, None] + col_sq[None, :] - 2.0 * cross
    return jnp.exp(dist * (-KERNEL_SCALE / features)).astype(jnp.bfloat16)


def sweep(row_pts, row_sq, col_pts, col_sq, panel, with_degree):
    rows, features = row_pts.shape
    height = min(512, rows)
    count = rows // height
    stacked = (row_pts.reshape(count, height, features), row_sq.reshape(count, height))

    def one_block(item):
        weights = affinity(item[0], item[1], col_pts, col_sq)
        results = ()
        if panel is not None:
            results = results + (jnp.dot(weights, panel, preferred_element_type=jnp.float32),)
        if with_degree:
            results = results + (jnp.sum(weights, axis=1, dtype=jnp.float32),)
        return results

    mapped = lax.map(one_block, stacked)
    return [piece.reshape((rows,) + piece.shape[2:]) for piece in mapped]


def orthonormal(product, degree, total):
    scaled = product / degree[:, None]
    gram_part = jnp.dot(
        scaled.T, scaled, precision=lax.Precision.HIGHEST, preferred_element_type=jnp.float32
    )
    gram = lax.psum(gram_part, ("row", "col"))
    lower = jnp.linalg.cholesky(gram / total)
    return lax.linalg.triangular_solve(lower, scaled, left_side=False, lower=True, transpose_a=True)


def shards(points, start_vectors):
    group = points.shape[0]
    total = group * lax.axis_size("row") * lax.axis_size("col")
    row_pts = lax.all_gather(points, "col", axis=0, tiled=True)
    col_pts = lax.all_gather(points, "row", axis=0, tiled=True)
    row_sq = squared_norms(row_pts)
    col_sq = squared_norms(col_pts)
    degree_part = sweep(row_pts, row_sq, col_pts, col_sq, None, True)[0]
    vectors = start_vectors
    ortho = jnp.zeros(start_vectors.shape, jnp.float32)
    degree = None
    for step in range(ITERS):
        panel = lax.all_gather(vectors, "row", axis=0, tiled=True)
        if step == 0:
            product_part = sweep(row_pts, row_sq, col_pts, col_sq, panel, False)[0]
            product, degree = (
                lax.psum_scatter(product_part, "col", scatter_dimension=0, tiled=True),
                lax.psum_scatter(degree_part, "col", scatter_dimension=0, tiled=True),
            )
        else:
            product_part = sweep(row_pts, row_sq, col_pts, col_sq, panel, False)[0]
            product = lax.psum_scatter(product_part, "col", scatter_dimension=0, tiled=True)
        ortho = orthonormal(product, degree, total)
        vectors = ortho.astype(jnp.bfloat16)
    return ortho


def solution(mesh):
    return jax.shard_map(
        shards,
        mesh=mesh,
        in_specs=(P(("row", "col"), None), P(("row", "col"), None)),
        out_specs=P(("row", "col"), None),
        check_vma=False,
    )
```

profile of v0, /device:TPU:10, one launch (start us, length us, event | category | flops | bytes accessed | tf_op | source)
XLA Modules:
  0.0 230.9 jit_solution(14613255640322226920)
XLA Ops:
  6.5 14.9 %all-gather = bf16[8,320,64]{1,2,0:T(8,128)(2,1)S(1)} all-gather(bf16[1,320,64]{1,2,0:T(8,128)(2,1)} %bitcast.101), channel_id=1, replica_groups=mesh['row'=4,'col'=8] {'col'}, dimensions={0}, use_global_device_ids=true | all-gather | bytes 368640 | tf_op jit(solution)/shard_map/all_gather | solution.py:55
  21.5 8.7 %all-gather.1 = bf16[4,320,64]{1,2,0:T(8,128)(2,1)S(1)} all-gather(bf16[1,320,64]{1,2,0:T(8,128)(2,1)} %bitcast.102), channel_id=1, replica_groups=mesh['row'=4,'col'=8] {'row'}, dimensions={0}, use_global_device_ids=true | all-gather | bytes 204800 | tf_op jit(solution)/shard_map/all_gather | solution.py:56
  31.3 7.6 %all-gather.2 = bf16[4,320,32]{1,2,0:T(8,128)(2,1)S(1)} all-gather(bf16[1,320,32]{1,2,0:T(8,128)(2,1)S(1)} %bitcast.107), channel_id=1, replica_groups=mesh['row'=4,'col'=8] {'row'}, dimensions={0}, use_global_device_ids=true | all-gather | bytes 102400 | tf_op jit(solution)/shard_map/all_gather | solution.py:64
  39.2 4.9 %while.30 = (s32[]{:T(128)}, f32[5,512,32]{1,2,0:T(8,128)S(1)}, f32[5,512]{1,0:T(8,128)S(1)}, f32[1280]{0:T(1024)S(1)}, bf16[5,512,64]{2,1,0:T(8,128)(2,1)S(1)},...) while((s32[]{:T(128)}, f32[5,512,32]{1,2,0:T(8,128)S(1)}, ...), condition=%wide.region_3.4_spmd, body=%wide.region_2.3_spmd.sunk | while | flops 129105920 | bytes 867417 | solution.py:38
  39.2 1.0 fusion.78
  40.2 1.0 fusion.78
  41.2 1.0 fusion.78
  42.2 1.0 fusion.78
  43.1 1.0 fusion.78
  44.1 1.5 copy.58
  45.7 4.8 %while.31 = (s32[]{:T(128)}, f32[5,512]{1,0:T(8,128)S(1)}, f32[5,512]{1,0:T(8,128)S(1)}, f32[1280]{0:T(1024)S(1)}, bf16[5,512,64]{2,1,0:T(8,128)(2,1)S(1)}, /*in...) while((s32[]{:T(128)}, f32[5,512]{1,0:T(8,128)S(1)}, f32[5,512]{1,0:T(8,128)S(1)}, f32[1280]{0:T(1024)S(1)}, ...), condition=%wide.region_7.8_spmd, body=%wide.region_5.7_spmd.sunk | while | flops 88473088 | bytes 479329 | solution.py:38
  45.7 0.9 fusion.81
  51.7 22.6 %all-reduce = f32[2560]{0:T(1024)S(1)} all-reduce(f32[2560]{0:T(1024)S(1)} %reshape.43), channel_id=3, replica_groups=mesh['row'=4,'col'=8] {'col'}, use_global_device_ids=true, to_apply=%region_8.9.clone | all-reduce | flops 2560 | bytes 20480
  74.4 1.8 reduce-scatter.7.cloned.1.call-done
  76.2 1.0 copy.52
  77.5 43.7 %psum.14 = f32[32,32]{0,1:T(8,128)S(1)} all-reduce(f32[32,32]{0,1:T(8,128)S(1)} %fusion.49), channel_id=1, replica_groups=mesh['row'=4,'col'=8] {'row','col'}, use_global_device_ids=true, to_apply=%region_9.10 | all-reduce | flops 1024 | bytes 8192 | tf_op jit(solution)/shard_map/psum | solution.py:47
  121.2 2.9 %cholesky.44 = f32[32,32]{1,0:T(8,128)S(1)} custom-call(f32[32,32]{1,0:T(8,128)S(1)} %fusion.56), custom_call_target="Cholesky" | custom-call | tf_op jit(solution)/shard_map/jit(cholesky)/cholesky | solution.py:48
  125.6 2.4 %custom-call.6 = f32[1,32,32]{1,2,0:T(8,128)S(1)} custom-call(f32[1,32,32]{2,1,0:T(8,128)S(1)} %fusion.51), custom_call_target="InvertDiagBlocksLowerTriangular" | custom-call | tf_op jit(solution)/shard_map/triangular_solve/custom-call.0 | solution.py:49
  128.3 7.6 %all-gather.3 = bf16[4,320,32]{1,2,0:T(8,128)(2,1)S(1)} all-gather(bf16[1,320,32]{1,2,0:T(8,128)(2,1)S(1)} %fusion.48), channel_id=1, replica_groups=mesh['row'=4,'col'=8] {'row'}, dimensions={0}, use_global_device_ids=true | all-gather | bytes 102400 | tf_op jit(solution)/shard_map/all_gather | solution.py:64
  136.1 4.9 %while.32 = (s32[]{:T(128)}, f32[5,512,32]{1,2,0:T(8,128)S(1)}, f32[5,512]{1,0:T(8,128)S(1)}, f32[1280]{0:T(1024)S(1)}, bf16[5,512,64]{2,1,0:T(8,128)(2,1)S(1)},...) while((s32[]{:T(128)}, f32[5,512,32]{1,2,0:T(8,128)S(1)}, ...), condition=%wide.region_13.16_spmd, body=%wide.region_12.15_spmd.sunk | while | flops 129105920 | bytes 867417 | solution.py:38
  136.2 1.0 fusion.85
  137.1 1.0 fusion.85
  138.1 1.0 fusion.85
  139.1 1.0 fusion.85
  140.1 1.0 fusion.85
  141.0 1.5 copy.60
  142.5 28.8 %reduce-scatter.9.cloned.1.call-done = f32[320,32]{1,0:T(8,128)} async-done(((f32[2560,32]{1,0:T(8,128)}), f32[320,32]{1,0:T(8,128)}) %reduce-scatter.9.cloned.1.call-update) | async-done | bytes 40976
  171.3 1.0 copy.54
  172.6 43.8 %psum.15 = f32[32,32]{0,1:T(8,128)S(1)} all-reduce(f32[32,32]{0,1:T(8,128)S(1)} %fusion.50), channel_id=1, replica_groups=mesh['row'=4,'col'=8] {'row','col'}, use_global_device_ids=true, to_apply=%region_15.18 | all-reduce | flops 1024 | bytes 8192 | tf_op jit(solution)/shard_map/psum | solution.py:47
  216.5 2.9 %cholesky.55 = f32[32,32]{1,0:T(8,128)S(1)} custom-call(f32[32,32]{1,0:T(8,128)S(1)} %fusion.54), custom_call_target="Cholesky" | custom-call | tf_op jit(solution)/shard_map/jit(cholesky)/cholesky | solution.py:48
  220.7 2.4 %custom-call.7 = f32[1,32,32]{1,2,0:T(8,128)S(1)} custom-call(f32[1,32,32]{2,1,0:T(8,128)S(1)} %fusion.52), custom_call_target="InvertDiagBlocksLowerTriangular" | custom-call | tf_op jit(solution)/shard_map/triangular_solve/custom-call.0 | solution.py:49
  223.1 0.9 convolution_bitcast_fusion
  (62 shorter events, 9.9 us)
Async XLA Ops:
  6.5 69.7 %reduce-scatter.7.cloned.1.call-start = ((), (), s32[]{:S(2)}) async-start(), calls=%async_computation.2 | async-start | bytes 1474560
  30.3 1.0 copy-start
  45.6 125.7 %reduce-scatter.9.cloned.1.call-start = ((), (), s32[]{:S(2)}) async-start(), calls=%async_computation.3 | async-start | bytes 1474560
  45.7 4.8 %copy-start.1 = (u32[32]{0:T(128)S(1)}, u32[32]{0:T(128)}, u32[]{:S(2)}) copy-start(u32[32]{0:T(128)} %constant.83) | copy-start | bytes 388
Sparse Core Ops, SparseCore 0:
  45.7 30.4 reduce-scatter.6
  142.7 28.6 reduce-scatter.8
where the time goes:
time: 231 us
  blocking collectives  149 us (65%)
  waiting for transfers between devices  30.6 us (13%)
  matrix products  15.5 us (7%)
  between operations  14.2 us (6%)
  other arithmetic  13.7 us (6%)
  local copies, waits for them, and re-layouts  7.7 us (3%)
    psum x2, blocking collectives, orthonormal(): gram = lax.psum(gram_part, ('row', 'col'))  87.5 us
    unnamed x4, waiting for transfers between devices  30.6 us
    unnamed x1, blocking collectives  22.6 us
    all_gather x2, blocking collectives, shards(): panel = lax.all_gather(vectors, 'row', axis=0, tiled=True)  15.2 us
    all_gather x1, blocking collectives, shards(): row_pts = lax.all_gather(points, 'col', axis=0, tiled=True)  14.9 us
    dot_general x10, matrix products, one_block(): jnp.dot(weights, panel, preferred_element_type=jnp.float32)  9.58 us
    all_gather x1, blocking collectives, shards(): col_pts = lax.all_gather(points, 'row', axis=0, tiled=True)  8.71 us
    another operation x6, other arithmetic, orthonormal(): lower = jnp.linalg.cholesky(gram / total)  7.27 us
  transfers between devices with their start and end apart: 2, of which 2 were waited for; matrix products, arithmetic and copies ran while one was open for 2% of the time, Pallas kernels for 0%

commit v1 on v0

--- a/solution.py
+++ b/solution.py
@@ -2,6 +2,7 @@
 import jax.numpy as jnp
 from jax import lax
 from jax.sharding import PartitionSpec as P
+from jax.lax import all_gather
 
 ITERS = 2
 KERNEL_SCALE = 5.12
@@ -44,7 +45,7 @@
     gram_part = jnp.dot(
         scaled.T, scaled, precision=lax.Precision.HIGHEST, preferred_element_type=jnp.float32
     )
-    gram = lax.psum(gram_part, ("row", "col"))
+    gram = jnp.sum(all_gather(gram_part, ("row", "col")), 0)
     lower = jnp.linalg.cholesky(gram / total)
     return lax.linalg.triangular_solve(lower, scaled, left_side=False, lower=True, transpose_a=True)
 

time: 231 us -> 232 us (level)
  the two profiles are of different devices: /device:TPU:10 before, /device:TPU:0 now
where the time goes in v1:
time: 232 us; the launch traced here: 231 us
  blocking collectives  147 us (63%)
  waiting for transfers between devices  33.1 us (14%)
  matrix products  15.5 us (7%)
  between operations  14.2 us (6%)
  other arithmetic  13.8 us (6%)
  local copies, waits for them, and re-layouts  7.83 us (3%)
    all_gather x2, blocking collectives, orthonormal(): gram = jnp.sum(all_gather(gram_part, ('row', 'col')), 0)  79.9 us
    unnamed x4, waiting for transfers between devices  33.1 us
    unnamed x1, blocking collectives  25.9 us
    all_gather x1, blocking collectives, shards(): row_pts = lax.all_gather(points, 'col', axis=0, tiled=True)  16.4 us
    all_gather x2, blocking collectives, shards(): panel = lax.all_gather(vectors, 'row', axis=0, tiled=True)  15.5 us
    dot_general x10, matrix products, one_block(): jnp.dot(weights, panel, preferred_element_type=jnp.float32)  9.6 us
    all_gather x1, blocking collectives, shards(): col_pts = lax.all_gather(points, 'row', axis=0, tiled=True)  8.96 us
    another operation x6, other arithmetic, orthonormal(): lower = jnp.linalg.cholesky(gram / total)  7.27 us
  transfers between devices with their start and end apart: 2, of which 2 were waited for; matrix products, arithmetic and copies ran while one was open for 2% of the time, Pallas kernels for 0%

profile of v1, /device:TPU:0, one launch (start us, length us, event | category | flops | bytes accessed | tf_op | source)
XLA Modules:
  0.0 231.4 jit_solution(12904690851949806799)
XLA Ops:
  6.5 16.4 %all-gather.2 = bf16[8,320,64]{1,2,0:T(8,128)(2,1)S(1)} all-gather(bf16[1,320,64]{1,2,0:T(8,128)(2,1)} %bitcast.105), channel_id=1, replica_groups=mesh['row'=4,'col'=8] {'col'}, dimensions={0}, use_global_device_ids=true | all-gather | bytes 368640 | tf_op jit(solution)/shard_map/all_gather | solution.py:56
  23.0 9.0 %all-gather.3 = bf16[4,320,64]{1,2,0:T(8,128)(2,1)S(1)} all-gather(bf16[1,320,64]{1,2,0:T(8,128)(2,1)} %bitcast.106), channel_id=1, replica_groups=mesh['row'=4,'col'=8] {'row'}, dimensions={0}, use_global_device_ids=true | all-gather | bytes 204800 | tf_op jit(solution)/shard_map/all_gather | solution.py:57
  33.1 8.1 %all-gather.4 = bf16[4,320,32]{1,2,0:T(8,128)(2,1)S(1)} all-gather(bf16[1,320,32]{1,2,0:T(8,128)(2,1)S(1)} %bitcast.111), channel_id=1, replica_groups=mesh['row'=4,'col'=8] {'row'}, dimensions={0}, use_global_device_ids=true | all-gather | bytes 102400 | tf_op jit(solution)/shard_map/all_gather | solution.py:65
  41.4 4.9 %while.30 = (s32[]{:T(128)}, f32[5,512,32]{1,2,0:T(8,128)S(1)}, f32[5,512]{1,0:T(8,128)S(1)}, f32[1280]{0:T(1024)S(1)}, bf16[5,512,64]{2,1,0:T(8,128)(2,1)S(1)},...) while((s32[]{:T(128)}, f32[5,512,32]{1,2,0:T(8,128)S(1)}, ...), condition=%wide.region_3.4_spmd, body=%wide.region_2.3_spmd.sunk | while | flops 129105920 | bytes 867417 | solution.py:39
  41.4 1.0 fusion.78
  42.4 1.0 fusion.78
  43.4 1.0 fusion.78
  44.4 1.0 fusion.78
  45.4 1.0 fusion.78
  46.3 1.5 copy.52
  47.9 4.8 %while.31 = (s32[]{:T(128)}, f32[5,512]{1,0:T(8,128)S(1)}, f32[5,512]{1,0:T(8,128)S(1)}, f32[1280]{0:T(1024)S(1)}, bf16[5,512,64]{2,1,0:T(8,128)(2,1)S(1)}, /*in...) while((s32[]{:T(128)}, f32[5,512]{1,0:T(8,128)S(1)}, f32[5,512]{1,0:T(8,128)S(1)}, f32[1280]{0:T(1024)S(1)}, ...), condition=%wide.region_7.8_spmd, body=%wide.region_5.7_spmd.sunk | while | flops 88473088 | bytes 479329 | solution.py:39
  49.8 0.9 fusion.81
  53.9 25.9 %all-reduce = f32[2560]{0:T(1024)S(1)} all-reduce(f32[2560]{0:T(1024)S(1)} %reshape.43), channel_id=5, replica_groups=mesh['row'=4,'col'=8] {'col'}, use_global_device_ids=true, to_apply=%region_8.9.clone | all-reduce | flops 2560 | bytes 20480
  79.9 1.5 reduce-scatter.7.cloned.1.call-done
  81.5 1.0 copy.46
  82.7 39.9 %all-gather = f32[1024,32]{1,0:T(8,128)S(1)} all-gather(f32[32,32]{1,0:T(8,128)S(1)} %fusion.49), channel_id=2, replica_groups=mesh['row'=4,'col'=8] {'row','col'}, dimensions={0}, use_global_device_ids=true | all-gather | bytes 135168 | tf_op jit(solution)/shard_map/all_gather | solution.py:48
  122.9 2.9 %cholesky.44 = f32[32,32]{1,0:T(8,128)S(1)} custom-call(f32[32,32]{1,0:T(8,128)S(1)} %fusion.56), custom_call_target="Cholesky" | custom-call | tf_op jit(solution)/shard_map/jit(cholesky)/cholesky | solution.py:49
  127.2 2.4 %custom-call.6 = f32[1,32,32]{1,2,0:T(8,128)S(1)} custom-call(f32[1,32,32]{2,1,0:T(8,128)S(1)} %fusion.51), custom_call_target="InvertDiagBlocksLowerTriangular" | custom-call | tf_op jit(solution)/shard_map/triangular_solve/custom-call.0 | solution.py:50
  130.0 7.4 %all-gather.5 = bf16[4,320,32]{1,2,0:T(8,128)(2,1)S(1)} all-gather(bf16[1,320,32]{1,2,0:T(8,128)(2,1)S(1)} %fusion.48), channel_id=1, replica_groups=mesh['row'=4,'col'=8] {'row'}, dimensions={0}, use_global_device_ids=true | all-gather | bytes 102400 | tf_op jit(solution)/shard_map/all_gather | solution.py:65
  137.7 4.9 %while.32 = (s32[]{:T(128)}, f32[5,512,32]{1,2,0:T(8,128)S(1)}, f32[5,512]{1,0:T(8,128)S(1)}, f32[1280]{0:T(1024)S(1)}, bf16[5,512,64]{2,1,0:T(8,128)(2,1)S(1)},...) while((s32[]{:T(128)}, f32[5,512,32]{1,2,0:T(8,128)S(1)}, ...), condition=%wide.region_13.16_spmd, body=%wide.region_12.15_spmd.sunk | while | flops 129105920 | bytes 867417 | solution.py:39
  137.7 1.0 fusion.85
  138.7 1.0 fusion.85
  139.6 1.0 fusion.85
  140.6 1.0 fusion.85
  141.6 1.0 fusion.85
  142.6 1.5 copy.54
  144.1 31.5 %reduce-scatter.9.cloned.1.call-done = f32[320,32]{1,0:T(8,128)} async-done(((f32[2560,32]{1,0:T(8,128)}), f32[320,32]{1,0:T(8,128)}) %reduce-scatter.9.cloned.1.call-update) | async-done | bytes 40976
  175.6 1.0 copy.48
  176.8 40.0 %all-gather.1 = f32[1024,32]{1,0:T(8,128)S(1)} all-gather(f32[32,32]{1,0:T(8,128)S(1)} %fusion.50), channel_id=3, replica_groups=mesh['row'=4,'col'=8] {'row','col'}, dimensions={0}, use_global_device_ids=true | all-gather | bytes 135168 | tf_op jit(solution)/shard_map/all_gather | solution.py:48
  217.0 2.9 %cholesky.55 = f32[32,32]{1,0:T(8,128)S(1)} custom-call(f32[32,32]{1,0:T(8,128)S(1)} %fusion.54), custom_call_target="Cholesky" | custom-call | tf_op jit(solution)/shard_map/jit(cholesky)/cholesky | solution.py:49
  221.2 2.4 %custom-call.7 = f32[1,32,32]{1,2,0:T(8,128)S(1)} custom-call(f32[1,32,32]{2,1,0:T(8,128)S(1)} %fusion.52), custom_call_target="InvertDiagBlocksLowerTriangular" | custom-call | tf_op jit(solution)/shard_map/triangular_solve/custom-call.0 | solution.py:50
  223.7 0.9 convolution_bitcast_fusion
  (66 shorter events, 10.1 us)
Async XLA Ops:
  6.5 74.9 %reduce-scatter.7.cloned.1.call-start = ((), (), s32[]{:S(2)}) async-start(), calls=%async_computation.2 | async-start | bytes 1474560
  32.1 1.0 copy-start
  47.8 127.8 %reduce-scatter.9.cloned.1.call-start = ((), (), s32[]{:S(2)}) async-start(), calls=%async_computation.3 | async-start | bytes 1474560
  47.9 4.8 %copy-start.1 = (u32[32]{0:T(128)S(1)}, u32[32]{0:T(128)}, u32[]{:S(2)}) copy-start(u32[32]{0:T(128)} %constant.83) | copy-start | bytes 388
Sparse Core Ops, SparseCore 0:
  47.9 33.4 reduce-scatter.6
  144.2 31.3 reduce-scatter.8
